TPU v7x, 32 devices: a whole 2x2x4 slice. The times are simulated.
32 devices in a mesh: dev: 8 (over z, y), rep: 4 (over x, core).
Axes of the slice: x: 2, y: 2, z: 4, core: 2. Of those that a mesh axis runs over, the one named last changes fastest.
Arguments:
- features: bfloat16 [32768, 256], P(('dev', 'rep')), may hold values from -6 to 6
- history: bfloat16 [32768, 256], P(('dev', 'rep')), may hold values from -6 to 6
- new_owner: int32 [32, 8], P(('dev', 'rep')), may hold values from 0 to 7, as said below
- pull_rows: int32 [32768], P(('dev', 'rep')), may hold values from 0 to 1023
- occupancy: int32 [256, 16], P(('dev', 'rep')), may hold values from 0 to 1, as said below
- adj_local: bfloat16 [32768, 1024], P(('dev', 'rep')), may hold values from -0.125 to 0.125
- adj_boundary: bfloat16 [32768, 1024], P(('dev', 'rep')), may hold values from -0.125 to 0.125
- w_first: bfloat16 [256, 256], replicated, may hold values from -0.375 to 0.375
- bias_first: float32 [256], replicated, may hold values from -3 to 3
- w_second: bfloat16 [256, 256], replicated, may hold values from -0.375 to 0.375
- cotangent: bfloat16 [32768, 256], P(('dev', 'rep')), may hold values from -6 to 6
Outputs:
- hidden: bfloat16 [32768, 256], P(('dev', 'rep'))
- output: bfloat16 [32768, 256], P(('dev', 'rep'))
- w_second_grad: float32 [256, 256], replicated
Inputs may be any that keep to these rules, and one draw needn't show every extreme that they name: Each row of new_owner is a permutation of 0 to 7. `occupancy`: tile flags of 0 or 1.
All inputs are finite; a program needn't handle non-finite values.
Results may differ from a plain program's by a relative error of at most 0.0061.
Values may be sent and summed in bfloat16 or wider, within the bound.
A program may use at most 64 MiB of HBM per device.

v0:
```python
import jax
import jax.numpy as jnp
from jax import lax
from jax.sharding import PartitionSpec as P


def expand(occupied):
    return jnp.repeat(jnp.repeat(occupied, 128, axis=0), 128, axis=1).astype(jnp.bfloat16)


def dense_terms(owned, remote, adj_local, adj_boundary, occupancy):
    height = owned.shape[0]
    full_mask = expand(occupancy)
    local_tile = adj_local * full_mask[:, :height]
    edge_tile = adj_boundary * full_mask[:, height:]
    summed = jnp.dot(local_tile, owned, preferred_element_type=jnp.float32)
    summed = summed + jnp.dot(edge_tile, remote, preferred_element_type=jnp.float32)
    partial_value = lax.dot_general(
        edge_tile, owned, (((0,), (0,)), ((), ())), preferred_element_type=jnp.float32
    )
    return (summed, partial_value)


def body(
    features,
    history,
    new_owner,
    pull_rows,
    occupancy,
    adj_local,
    adj_boundary,
    w_first,
    bias_first,
    w_second,
    cotangent,
):
    peer_count = lax.axis_size("dev")
    height, breadth = features.shape
    cluster = height // peer_count
    pulled = pull_rows.shape[0]
    per_peer = pulled // peer_count
    indices = jnp.arange(peer_count, dtype=jnp.int32)
    matches = (new_owner[0][:, None] == indices[None, :]).astype(jnp.int32)
    inverse = jnp.sum(matches * indices[:, None], axis=0)

    def arrange(values):
        return values.reshape(peer_count, cluster, breadth)[inverse]

    requests = lax.all_to_all(
        pull_rows.reshape(peer_count, per_peer), "dev", split_axis=0, concat_axis=0, tiled=True
    ).reshape(pulled)

    def fetch_rows(values):
        return values[requests].reshape(peer_count, per_peer, breadth)

    selector = (requests[None, :] == jnp.arange(height, dtype=jnp.int32)[:, None]).astype(
        jnp.bfloat16
    )

    def collect(received):
        return jnp.dot(
            selector, received.reshape(pulled, breadth), preferred_element_type=jnp.float32
        )

    def layer_terms(owned, remote):
        return dense_terms(owned, remote, adj_local, adj_boundary, occupancy)

    moved_x, moved_h = (
        lax.all_to_all(arrange(features), "dev", split_axis=0, concat_axis=0, tiled=True),
        lax.all_to_all(arrange(history), "dev", split_axis=0, concat_axis=0, tiled=True),
    )
    own_x = moved_x.reshape(height, breadth)
    own_h = moved_h.reshape(height, breadth)
    far_x, far_h = (
        lax.all_to_all(fetch_rows(own_x), "dev", split_axis=0, concat_axis=0, tiled=True),
        lax.all_to_all(fetch_rows(own_h), "dev", split_axis=0, concat_axis=0, tiled=True),
    )
    summed_one, partial_one = layer_terms(own_x, far_x.reshape(pulled, breadth))
    pushed_one = lax.all_to_all(
        partial_one.astype(jnp.bfloat16).reshape(peer_count, per_peer, breadth),
        "dev",
        split_axis=0,
        concat_axis=0,
        tiled=True,
    )
    far_h = far_h.reshape(pulled, breadth)
    aggregate_one = (summed_one + collect(pushed_one)).astype(jnp.bfloat16)
    hidden = jnp.maximum(
        jnp.dot(aggregate_one, w_first, preferred_element_type=jnp.float32) + bias_first, 0.0
    ).astype(jnp.bfloat16)
    summed_two, partial_two = layer_terms(hidden, far_h)
    pushed_two = lax.all_to_all(
        partial_two.astype(jnp.bfloat16).reshape(peer_count, per_peer, breadth),
        "dev",
        split_axis=0,
        concat_axis=0,
        tiled=True,
    )
    aggregate_two = (summed_two + collect(pushed_two)).astype(jnp.bfloat16)
    output = jnp.dot(aggregate_two, w_second, preferred_element_type=jnp.float32).astype(
        jnp.bfloat16
    )
    local_grad = lax.dot_general(
        aggregate_two, cotangent, (((0,), (0,)), ((), ())), preferred_element_type=jnp.float32
    )
    gradient = lax.psum(local_grad, ("dev", "rep"))
    return (hidden, output, gradient)


def solution(mesh):
    return jax.shard_map(
        body,
        mesh=mesh,
        in_specs=(
            P(("dev", "rep"), None),
            P(("dev", "rep"), None),
            P(("dev", "rep"), None),
            P(("dev", "rep")),
            P(("dev", "rep"), None),
            P(("dev", "rep"), None),
            P(("dev", "rep"), None),
            P(),
            P(),
            P(),
            P(("dev", "rep"), None),
        ),
        out_specs=(P(("dev", "rep"), None), P(("dev", "rep"), None), P()),
        check_vma=False,
    )
```

profile of v0, /device:TPU:0, one launch (start us, length us, event | category | flops | bytes accessed | tf_op | source)
XLA Modules:
  0.0 263.3 jit_solution(17940252568643423680)
XLA Ops:
  7.2 7.5 %all-to-all-start.1 = ((s32[8,1,128]{2,1,0:T(1,128)}), s32[8,1,128]{2,1,0:T(1,128)S(1)}, u32[]{:S(2)}, u32[]{:S(2)}) async-start(s32[8,1,128]{2,1,0:T(1,128)} %bitcast.62), calls=%async_computation.1 | async-start | bytes 8192 | tf_op jit(solution)/shard_map/all_to_all | solution.py:49
  15.4 1.4 gather_fusion
  16.8 4.3 %all-to-all-done.1 = s32[8,1,128]{2,1,0:T(1,128)S(1)} async-done(((s32[8,1,128]{2,1,0:T(1,128)}), s32[8,1,128]{2,1,0:T(1,128)S(1)}, u32[]{:S(2)}, u32[]{:S(2)}) %all-to-all-start.1) | async-done | bytes 4128 | tf_op jit(solution)/shard_map/all_to_all | solution.py:49
  21.1 3.5 %all-to-all-start = ((bf16[8,128,256]{2,1,0:T(8,128)(2,1)}), bf16[8,128,256]{2,1,0:T(8,128)(2,1)S(1)}, u32[]{:S(2)}, u32[]{:S(2)}) async-start(bf16[8,128,256]{2,1,0:T(8,128)(2,1)} %gather_fusion), calls=%async_computation | async-start | bytes 1048576 | tf_op jit(solution)/shard_map/all_to_all | solution.py:69
  24.6 1.4 gather_fusion.2
  25.9 11.9 %all-to-all-done = bf16[8,128,256]{2,1,0:T(8,128)(2,1)S(1)} async-done(((bf16[8,128,256]{2,1,0:T(8,128)(2,1)}), bf16[8,128,256]{2,1,0:T(8,128)(2,1)S(1)}, u32[]{:S(2)}, u32[]{:S(2)}) %all-to-all-start) | async-done | bytes 524320 | tf_op jit(solution)/shard_map/all_to_all | solution.py:69
  37.8 3.7 %all-to-all-start.4 = ((bf16[8,128,256]{2,1,0:T(8,128)(2,1)}), bf16[8,128,256]{2,1,0:T(8,128)(2,1)S(1)}, u32[]{:S(2)}, u32[]{:S(2)}) async-start(bf16[8,128,256]{2,1,0:T(8,128)(2,1)} %gather_fusion.2), calls=%async_computation.4 | async-start | bytes 1048576 | tf_op jit(solution)/shard_map/all_to_all | solution.py:70
  41.5 5.0 %gather_fusion.1 = bf16[1024,256]{1,0:T(8,128)(2,1)} fusion(bf16[1024,256]{1,0:T(8,128)(2,1)S(1)} %bitcast.45, s32[1024]{0:T(1024)S(1)} %broadcast_clamp_fusion), kind=kCustom, calls=%fused_computation.1 | custom fusion | bytes 1052672 | tf_op jit(solution)/shard_map/gather | solution.py:54
  46.5 8.8 %all-to-all-done.4 = bf16[8,128,256]{2,1,0:T(8,128)(2,1)S(1)} async-done(((bf16[8,128,256]{2,1,0:T(8,128)(2,1)}), bf16[8,128,256]{2,1,0:T(8,128)(2,1)S(1)}, u32[]{:S(2)}, u32[]{:S(2)}) %all-to-all-start.4) | async-done | bytes 524320 | tf_op jit(solution)/shard_map/all_to_all | solution.py:70
  55.3 4.2 %all-to-all-start.2 = ((bf16[8,128,256]{2,1,0:T(8,128)(2,1)}), bf16[8,128,256]{2,1,0:T(8,128)(2,1)}, u32[]{:S(2)}, u32[]{:S(2)}) async-start(bf16[8,128,256]{2,1,0:T(8,128)(2,1)} %bitcast.9), calls=%async_computation.2 | async-start | bytes 1048576 | tf_op jit(solution)/shard_map/all_to_all | solution.py:75
  59.5 4.5 %broadcast_in_dim.5 = bf16[1024,16,128]{2,1,0:T(8,128)(2,1)S(1)} broadcast(bf16[1024,16]{1,0:T(8,128)(2,1)S(1)} %bitcast.55), dimensions={0,1} | broadcast | bytes 4227072 | tf_op jit(solution)/shard_map/broadcast_in_dim | solution.py:8
  64.0 2.2 copy.16
  66.4 1.7 copy-done.2
  68.1 1.6 convolution_convert_fusion.2
  69.7 3.5 %all-to-all-done.2 = bf16[8,128,256]{2,1,0:T(8,128)(2,1)} async-done(((bf16[8,128,256]{2,1,0:T(8,128)(2,1)}), bf16[8,128,256]{2,1,0:T(8,128)(2,1)}, u32[]{:S(2)}, u32[]{:S(2)}) %all-to-all-start.2) | async-done | bytes 524320 | tf_op jit(solution)/shard_map/all_to_all | solution.py:75
  73.2 4.1 %all-to-all-start.3 = ((bf16[8,128,256]{2,1,0:T(8,128)(2,1)}), bf16[8,128,256]{2,1,0:T(8,128)(2,1)}, u32[]{:S(2)}, u32[]{:S(2)}) async-start(bf16[8,128,256]{2,1,0:T(8,128)(2,1)} %bitcast.57), calls=%async_computation.3 | async-start | bytes 1048576 | tf_op jit(solution)/shard_map/all_to_all | solution.py:79
  77.4 5.7 %gather_fusion.3 = bf16[1024,256]{1,0:T(8,128)(2,1)} fusion(bf16[1024,256]{1,0:T(8,128)(2,1)} %bitcast.48, s32[1024]{0:T(1024)S(1)} %broadcast_clamp_fusion), kind=kCustom, calls=%fused_computation.3 | custom fusion | bytes 1052672 | tf_op jit(solution)/shard_map/gather | solution.py:54
  83.1 3.9 %fusion.11 = f32[1024,256]{1,0:T(8,128)} fusion(bf16[1024,256]{1,0:T(8,128)(2,1)S(1)} %bitcast.47, bf16[1024,1024]{1,0:T(8,128)(2,1)} %param.16, bf16[1024,2048]{1,0:T(8,128)(2,1)} %bitcast.51), kind=kOutput, calls=%fused_computation.25 | convolution fusion | flops 537919488 | bytes 5767168 | tf_op jit(solution)/shard_map/dot_general | solution.py:16
  87.0 3.7 %all-to-all-done.3 = bf16[8,128,256]{2,1,0:T(8,128)(2,1)} async-done(((bf16[8,128,256]{2,1,0:T(8,128)(2,1)}), bf16[8,128,256]{2,1,0:T(8,128)(2,1)}, u32[]{:S(2)}, u32[]{:S(2)}) %all-to-all-start.3) | async-done | bytes 524320 | tf_op jit(solution)/shard_map/all_to_all | solution.py:79
  90.7 3.7 %all-to-all-start.5 = ((bf16[8,128,256]{2,1,0:T(8,128)(2,1)}), bf16[8,128,256]{2,1,0:T(8,128)(2,1)S(1)}, u32[]{:S(2)}, u32[]{:S(2)}) async-start(bf16[8,128,256]{2,1,0:T(8,128)(2,1)} %bitcast.53), calls=%async_computation.5 | async-start | bytes 1048576 | tf_op jit(solution)/shard_map/all_to_all | solution.py:76
  94.4 3.1 %convolution_add_fusion.2 = f32[1024,256]{1,0:T(8,128)} fusion(f32[1024,256]{1,0:T(8,128)} %fusion.11, bf16[1024,1024]{1,0:T(8,128)(2,1)S(1)} %slice_multiply_fusion, bf16[1024,256]{1,0:T(8,128)(2,1)} %bitcast.10), kind=kOutput, calls=%fused_computation.17 | convolution fusion | flops 537133056 | bytes 4718592 | tf_op jit(solution)/shard_map/dot_general | solution.py:17
  97.5 3.2 %fusion.7 = bf16[1024,256]{1,0:T(8,128)(2,1)} fusion(bf16[256,256]{1,0:T(8,128)(2,1)S(1)} %copy-done.8, f32[1024,256]{1,0:T(8,128)} %convolution_add_fusion.2, bf16[1024,256]{1,0:T(8,128)(2,1)} %bitcast.13, s32[1024]{0:T(1024)S(1)} %bitcast.59, f32[256]{0:T(256)S(1)} %copy-done.9), kind=kOutput, calls=%fused_computation.18 | convolution fusion | flops 673447936 | bytes 2233344 | tf_op jit(solution)/shard_map/dot_general | solution.py:89
  100.7 2.6 convolution_convert_fusion.1
  103.3 4.8 %all-to-all-done.5 = bf16[8,128,256]{2,1,0:T(8,128)(2,1)S(1)} async-done(((bf16[8,128,256]{2,1,0:T(8,128)(2,1)}), bf16[8,128,256]{2,1,0:T(8,128)(2,1)S(1)}, u32[]{:S(2)}, u32[]{:S(2)}) %all-to-all-start.5) | async-done | bytes 524320 | tf_op jit(solution)/shard_map/all_to_all | solution.py:76
  108.2 4.1 %all-to-all-start.6 = ((bf16[8,128,256]{2,1,0:T(8,128)(2,1)}), bf16[8,128,256]{2,1,0:T(8,128)(2,1)}, u32[]{:S(2)}, u32[]{:S(2)}) async-start(bf16[8,128,256]{2,1,0:T(8,128)(2,1)} %bitcast.56), calls=%async_computation.6 | async-start | bytes 1048576 | tf_op jit(solution)/shard_map/all_to_all | solution.py:92
  112.5 3.0 %fusion.10 = f32[1024,256]{1,0:T(8,128)S(1)} fusion(bf16[1024,256]{1,0:T(8,128)(2,1)} %fusion.7, bf16[1024,1024]{1,0:T(8,128)(2,1)} %param.16, bf16[1024,2048]{1,0:T(8,128)(2,1)} %bitcast.52), kind=kOutput, calls=%fused_computation.24 | convolution fusion | flops 537919488 | bytes 5767168 | tf_op jit(solution)/shard_map/dot_general | solution.py:16
  115.6 1.7 convolution_add_fusion.1
  117.3 8.4 %all-to-all-done.6 = bf16[8,128,256]{2,1,0:T(8,128)(2,1)} async-done(((bf16[8,128,256]{2,1,0:T(8,128)(2,1)}), bf16[8,128,256]{2,1,0:T(8,128)(2,1)}, u32[]{:S(2)}, u32[]{:S(2)}) %all-to-all-start.6) | async-done | bytes 524320 | tf_op jit(solution)/shard_map/all_to_all | solution.py:92
  125.7 2.2 fusion.8
  129.0 1.1 convolution_convert_fusion
  130.1 124.7 %all-reduce.2.cloned.1.call-done = f32[256,256]{1,0:T(8,128)} async-done(((f32[256,256]{1,0:T(8,128)}), f32[256,256]{1,0:T(8,128)}) %all-reduce.2.cloned.1.call-update) | async-done | bytes 262160 | tf_op jit(solution)/shard_map/psum | solution.py:106
  254.8 1.7 copy.18
  (30 shorter events, 2.4 us)
Async XLA Ops:
  7.2 8.2 %copy-start = (bf16[1024,256]{1,0:T(8,128)(2,1)S(1)}, bf16[1024,256]{1,0:T(8,128)(2,1)}, u32[]{:S(2)}) copy-start(bf16[1024,256]{1,0:T(8,128)(2,1)} %param.11) | copy-start | bytes 1572868
  7.2 17.4 %copy-start.5 = (bf16[1024,256]{1,0:T(8,128)(2,1)S(1)}, bf16[1024,256]{1,0:T(8,128)(2,1)}, u32[]{:S(2)}) copy-start(bf16[1024,256]{1,0:T(8,128)(2,1)} %param.12) | copy-start | bytes 1572868
  7.2 13.9 %all-to-all-start.1 = ((s32[8,1,128]{2,1,0:T(1,128)}), s32[8,1,128]{2,1,0:T(1,128)S(1)}, u32[]{:S(2)}, u32[]{:S(2)}) async-start(s32[8,1,128]{2,1,0:T(1,128)} %bitcast.62), calls=%async_computation.1 | async-start | bytes 8192 | tf_op jit(solution)/shard_map/all_to_all | solution.py:49
  21.1 16.8 %all-to-all-start = ((bf16[8,128,256]{2,1,0:T(8,128)(2,1)}), bf16[8,128,256]{2,1,0:T(8,128)(2,1)S(1)}, u32[]{:S(2)}, u32[]{:S(2)}) async-start(bf16[8,128,256]{2,1,0:T(8,128)(2,1)} %gather_fusion), calls=%async_computation | async-start | bytes 1048576 | tf_op jit(solution)/shard_map/all_to_all | solution.py:69
  37.8 17.5 %all-to-all-start.4 = ((bf16[8,128,256]{2,1,0:T(8,128)(2,1)}), bf16[8,128,256]{2,1,0:T(8,128)(2,1)S(1)}, u32[]{:S(2)}, u32[]{:S(2)}) async-start(bf16[8,128,256]{2,1,0:T(8,128)(2,1)} %gather_fusion.2), calls=%async_computation.4 | async-start | bytes 1048576 | tf_op jit(solution)/shard_map/all_to_all | solution.py:70
  41.5 18.0 %copy-start.7 = (s32[8,16]{1,0:T(8,128)S(1)}, s32[8,16]{1,0:T(8,128)}, u32[]{:S(2)}) copy-start(s32[8,16]{1,0:T(8,128)} %param.15) | copy-start | bytes 1540
  55.3 8.7 %copy-start.1 = (bf16[8,128,256]{2,1,0:T(8,128)(2,1)}, bf16[8,128,256]{2,1,0:T(8,128)(2,1)S(1)}, u32[]{:S(2)}) copy-start(bf16[8,128,256]{2,1,0:T(8,128)(2,1)S(1)} %all-to-all-done.4) | copy-start | bytes 1572868
  55.3 17.9 %all-to-all-start.2 = ((bf16[8,128,256]{2,1,0:T(8,128)(2,1)}), bf16[8,128,256]{2,1,0:T(8,128)(2,1)}, u32[]{:S(2)}, u32[]{:S(2)}) async-start(bf16[8,128,256]{2,1,0:T(8,128)(2,1)} %bitcast.9), calls=%async_computation.2 | async-start | bytes 1048576 | tf_op jit(solution)/shard_map/all_to_all | solution.py:75
  64.0 2.2 copy-start.3
  66.2 1.9 copy-start.2
  73.2 17.5 %all-to-all-start.3 = ((bf16[8,128,256]{2,1,0:T(8,128)(2,1)}), bf16[8,128,256]{2,1,0:T(8,128)(2,1)}, u32[]{:S(2)}, u32[]{:S(2)}) async-start(bf16[8,128,256]{2,1,0:T(8,128)(2,1)} %bitcast.57), calls=%async_computation.3 | async-start | bytes 1048576 | tf_op jit(solution)/shard_map/all_to_all | solution.py:79
  90.7 17.5 %all-to-all-start.5 = ((bf16[8,128,256]{2,1,0:T(8,128)(2,1)}), bf16[8,128,256]{2,1,0:T(8,128)(2,1)S(1)}, u32[]{:S(2)}, u32[]{:S(2)}) async-start(bf16[8,128,256]{2,1,0:T(8,128)(2,1)} %bitcast.53), calls=%async_computation.5 | async-start | bytes 1048576 | tf_op jit(solution)/shard_map/all_to_all | solution.py:76
  94.4 3.1 %copy-start.8 = (bf16[256,256]{1,0:T(8,128)(2,1)S(1)}, bf16[256,256]{1,0:T(8,128)(2,1)}, u32[]{:S(2)}) copy-start(bf16[256,256]{1,0:T(8,128)(2,1)} %param.18) | copy-start | bytes 393220
  94.4 3.1 %copy-start.9 = (f32[256]{0:T(256)S(1)}, f32[256]{0:T(256)}, u32[]{:S(2)}) copy-start(f32[256]{0:T(256)} %param.19) | copy-start | bytes 3076
  108.2 17.5 %all-to-all-start.6 = ((bf16[8,128,256]{2,1,0:T(8,128)(2,1)}), bf16[8,128,256]{2,1,0:T(8,128)(2,1)}, u32[]{:S(2)}, u32[]{:S(2)}) async-start(bf16[8,128,256]{2,1,0:T(8,128)(2,1)} %bitcast.56), calls=%async_computation.6 | async-start | bytes 1048576 | tf_op jit(solution)/shard_map/all_to_all | solution.py:92
  112.3 142.5 %all-reduce.2.cloned.1.call-start = ((), (), s32[]{:S(2)}) async-start(), calls=%async_computation.7 | async-start | bytes 524288 | tf_op jit(solution)/shard_map/psum | solution.py:106
  117.3 10.7 %copy-start.4 = (bf16[1024,256]{1,0:T(8,128)(2,1)S(1)}, bf16[1024,256]{1,0:T(8,128)(2,1)}, u32[]{:S(2)}) copy-start(bf16[1024,256]{1,0:T(8,128)(2,1)} %param.21) | copy-start | bytes 1572868
  125.7 3.3 %copy-start.6 = (bf16[256,256]{1,0:T(8,128)(2,1)S(1)}, bf16[256,256]{1,0:T(8,128)(2,1)}, u32[]{:S(2)}) copy-start(bf16[256,256]{1,0:T(8,128)(2,1)} %param.20) | copy-start | bytes 393220
Sparse Core Ops, SparseCore 0:
  129.1 125.6 all-reduce.1
where the time goes:
time: 264 us; the launch traced here: 263 us
  waiting for transfers between devices  170 us (64%)
  starting transfers between devices  31 us (12%)
  local copies, waits for them, and re-layouts  23.5 us (9%)
  matrix products  23.5 us (9%)
  between operations  14.2 us (5%)
    psum x1, waiting for transfers between devices, body(): gradient = lax.psum(local_grad, ('dev', 'rep'))  125 us
    all_to_all x1, waiting for transfers between devices, body(): lax.all_to_all(arrange(features), 'dev', split_axis=0, concat_axis=0, til...  11.9 us
    gather x2, local copies, waits for them, and re-layouts, fetch_rows(): return values[requests].reshape(peer_count, per_peer, breadth)  10.7 us
    all_to_all x1, waiting for transfers between devices, body(): lax.all_to_all(arrange(history), 'dev', split_axis=0, concat_axis=0, tile...  8.81 us
    all_to_all x1, waiting for transfers between devices, body(): lax.all_to_all(partial_two.astype(jnp.bfloat16).reshape(peer_count, per_p...  8.41 us
    all_to_all x1, starting transfers between devices, body(): lax.all_to_all(pull_rows.reshape(peer_count, per_peer), 'dev', split_axis...  7.45 us
    dot_general x2, matrix products, dense_terms(): summed = jnp.dot(local_tile, owned, preferred_element_type=jnp.float32)  6.92 us
    unnamed x22, local copies, waits for them, and re-layouts  5.58 us
  transfers between devices with their start and end apart: 8, of which 8 were waited for; matrix products, arithmetic and copies ran while one was open for 16% of the time, Pallas kernels for 0%

commit v1 on v0

--- a/solution.py
+++ b/solution.py
@@ -1,7 +1,426 @@
+import functools
+
 import jax
 import jax.numpy as jnp
 from jax import lax
+from jax.experimental import pallas as pl
+from jax.experimental.pallas import tpu as pltpu
 from jax.sharding import PartitionSpec as P
+
+MESH = pl.DeviceIdType.MESH
+F32 = jnp.float32
+BF16 = jnp.bfloat16
+ASK, MOVE_X, MOVE_H, FAR_X, FAR_H, PUSH_ONE, PUSH_TWO, SCATTER, GATHER = range(9)
+
+
+def step_kernel(
+    n,
+    reps,
+    features,
+    history,
+    new_owner,
+    pulls,
+    occupancy,
+    adj_local_hbm,
+    adj_edge_hbm,
+    w_first,
+    bias_first,
+    w_second,
+    cotangent_hbm,
+    hidden_out,
+    output_out,
+    grad_out,
+    local,
+    edge,
+    edge_t,
+    cotangent,
+    asked,
+    pick,
+    pick_t,
+    send_x,
+    send_h,
+    own_x,
+    own_h,
+    send_far_x,
+    send_far_h,
+    far_x,
+    far_h,
+    send_one,
+    send_two,
+    push_one,
+    push_two,
+    acc,
+    hidden,
+    agg,
+    grad_mine,
+    grad_rep,
+    sum_rep,
+    grad_dev,
+    sum_dev,
+    grad_rows,
+    grad_all,
+    load_sem,
+    send_sem,
+    recv_sem,
+    rep_send,
+    rep_recv,
+):
+    me = lax.axis_index("dev")
+    my_rep = lax.axis_index("rep")
+    height, breadth = features.shape
+    cluster = height // n
+    per_peer = pulls.shape[2]
+    pulled = n * per_peer
+    tile = height // occupancy.shape[0]
+    band = min(256, height)
+
+    def peer(off):
+        return lax.rem(me + off, n)
+
+    def rep_peer(off):
+        return lax.rem(my_rep + off, reps)
+
+    loads = [
+        pltpu.make_async_copy(adj_edge_hbm, edge, load_sem.at[0]),
+        pltpu.make_async_copy(adj_local_hbm, local, load_sem.at[1]),
+        pltpu.make_async_copy(cotangent_hbm, cotangent, load_sem.at[2]),
+    ]
+    for load in loads:
+        load.start()
+
+    barrier = pltpu.get_barrier_semaphore()
+    for off in range(1, n):
+        pl.semaphore_signal(barrier, inc=1, device_id={"dev": peer(off)}, device_id_type=MESH)
+    for off in range(1, reps):
+        pl.semaphore_signal(barrier, inc=1, device_id={"rep": rep_peer(off)}, device_id_type=MESH)
+
+    def cluster_for(source, owner):
+        block = jnp.zeros((cluster, breadth), BF16)
+        for j in range(n):
+            chosen = jnp.where(new_owner[0, j] == owner, 1.0, 0.0)
+            weight = jnp.full((cluster, breadth), chosen, F32).astype(BF16)
+            block = block + source[j * cluster : (j + 1) * cluster, :] * weight
+        return block
+
+    def outgoing(phase, src, dst, to, slot):
+        return pltpu.make_async_remote_copy(
+            src_ref=src.at[to],
+            dst_ref=dst.at[slot],
+            send_sem=send_sem.at[phase, to],
+            recv_sem=recv_sem.at[phase, slot],
+            device_id={"dev": to},
+            device_id_type=MESH,
+        )
+
+    def send(phase, src, dst, off):
+        outgoing(phase, src, dst, peer(off), me).start()
+
+    def receive(phase, src, dst):
+        for off in range(1, n):
+            other = peer(off)
+            outgoing(phase, src, dst, other, other).wait_recv()
+
+    def finish(phase, src, dst):
+        for off in range(1, n):
+            outgoing(phase, src, dst, peer(off), me).wait_send()
+
+    for off in range(1, n):
+        send_x[peer(off)] = cluster_for(features, peer(off))
+    own_x[me] = cluster_for(features, me)
+    pl.semaphore_wait(barrier, n - 1 + reps - 1)
+    for off in range(1, n):
+        send(ASK, pulls, asked, off)
+    for off in range(1, n):
+        send(MOVE_X, send_x, own_x, off)
+    for off in range(1, n):
+        send_h[peer(off)] = cluster_for(history, peer(off))
+        send(MOVE_H, send_h, own_h, off)
+    own_h[me] = cluster_for(history, me)
+    asked[me] = pulls[me]
+
+    loads[0].wait()
+    for i in range(height // tile):
+        for j in range(pulled // tile):
+            kept = occupancy[i, height // tile + j].astype(F32)
+            rows, cols = pl.ds(i * tile, tile), pl.ds(j * tile, tile)
+            part = (edge[rows, cols].astype(F32) * kept).astype(BF16)
+            edge[rows, cols] = part
+            edge_t[cols, rows] = part.T
+    loads[1].wait()
+    for i in range(height // tile):
+        for j in range(height // tile):
+            kept = occupancy[i, j].astype(F32)
+            rows, cols = pl.ds(i * tile, tile), pl.ds(j * tile, tile)
+            local[rows, cols] = (local[rows, cols].astype(F32) * kept).astype(BF16)
+
+    receive(ASK, pulls, asked)
+    for d in range(n):
+        wanted = asked[d]
+        rows = lax.broadcasted_iota(jnp.int32, (height, per_peer), 0)
+        pick[:, d * per_peer : (d + 1) * per_peer] = jnp.where(rows == wanted, 1.0, 0.0).astype(
+            BF16
+        )
+        turned = jnp.broadcast_to(wanted, (per_peer, per_peer)).T
+        lanes = lax.broadcasted_iota(jnp.int32, (per_peer, per_peer), 1)
+        for c in range(height // per_peer):
+            pick_t[d * per_peer : (d + 1) * per_peer, c * per_peer : (c + 1) * per_peer] = (
+                jnp.where(turned == lanes + c * per_peer, 1.0, 0.0).astype(BF16)
+            )
+
+    def blocks_out(phase, left, right, src, dst):
+        values = right[...].reshape(left.shape[1], breadth)
+
+        def block(to):
+            rows = pl.ds(pl.multiple_of(to * per_peer, per_peer), per_peer)
+            return jnp.dot(left[rows, :], values, preferred_element_type=F32).astype(BF16)
+
+        def one(off, carry):
+            src[peer(off)] = block(peer(off))
+            send(phase, src, dst, off)
+            return carry
+
+        lax.fori_loop(1, n, one, 0)
+        dst[me] = block(me)
+
+    def bands(body):
+        def one(i, carry):
+            body(pl.ds(pl.multiple_of(i * band, band), band))
+            return carry
+
+        lax.fori_loop(0, height // band, one, 0)
+
+    def times(left, rows, right):
+        values = right[...].reshape(left.shape[1], breadth)
+        return jnp.dot(left[rows, :], values, preferred_element_type=F32)
+
+    receive(MOVE_X, send_x, own_x)
+    blocks_out(FAR_X, pick_t, own_x, send_far_x, far_x)
+    blocks_out(PUSH_ONE, edge_t, own_x, send_one, push_one)
+
+    def local_one(rows):
+        acc[rows, :] = times(local, rows, own_x)
+
+    bands(local_one)
+    receive(MOVE_H, send_h, own_h)
+    blocks_out(FAR_H, pick_t, own_h, send_far_h, far_h)
+    receive(FAR_X, send_far_x, far_x)
+
+    def edge_one(rows):
+        acc[rows, :] = acc[rows, :] + times(edge, rows, far_x)
+
+    bands(edge_one)
+    receive(PUSH_ONE, send_one, push_one)
+
+    def first(rows):
+        total = (acc[rows, :] + times(pick, rows, push_one)).astype(BF16)
+        value = jnp.dot(total, w_first[...], preferred_element_type=F32) + bias_first[...]
+        value = jnp.maximum(value, 0.0).astype(BF16)
+        hidden[rows, :] = value
+        hidden_out[rows, :] = value
+
+    bands(first)
+    blocks_out(PUSH_TWO, edge_t, hidden, send_two, push_two)
+
+    def local_two(rows):
+        acc[rows, :] = times(local, rows, hidden)
+
+    bands(local_two)
+    receive(FAR_H, send_far_h, far_h)
+
+    def edge_two(rows):
+        acc[rows, :] = acc[rows, :] + times(edge, rows, far_h)
+
+    bands(edge_two)
+    loads[2].wait()
+    receive(PUSH_TWO, send_two, push_two)
+
+    def second(rows):
+        agg[rows, :] = (acc[rows, :] + times(pick, rows, push_two)).astype(BF16)
+
+    bands(second)
+    grad = lax.dot_general(
+        agg[...], cotangent[...], (((0,), (0,)), ((), ())), preferred_element_type=F32
+    )
+    grad_mine[...] = grad.reshape(grad_mine.shape)
+
+    def across(phase, src, dst, to, slot):
+        return pltpu.make_async_remote_copy(
+            src_ref=src,
+            dst_ref=dst.at[slot],
+            send_sem=rep_send.at[phase, to],
+            recv_sem=rep_recv.at[phase, slot],
+            device_id={"rep": to},
+            device_id_type=MESH,
+        )
+
+    def share(src, dst, to, slot):
+        return pltpu.make_async_remote_copy(
+            src_ref=src,
+            dst_ref=dst.at[slot],
+            send_sem=send_sem.at[GATHER, to],
+            recv_sem=recv_sem.at[GATHER, slot],
+            device_id={"dev": to},
+            device_id_type=MESH,
+        )
+
+    for off in range(1, reps):
+        to = rep_peer(off)
+        across(0, grad_mine.at[to], grad_rep, to, my_rep).start()
+
+    def last(rows):
+        output_out[rows, :] = jnp.dot(
+            agg[rows, :], w_second[...], preferred_element_type=F32
+        ).astype(BF16)
+
+    bands(last)
+    total = grad_mine[my_rep]
+    for off in range(1, reps):
+        to = rep_peer(off)
+        across(0, grad_mine.at[to], grad_rep, to, to).wait_recv()
+        total = total + grad_rep[to]
+    sum_rep[...] = total
+    for off in range(1, n):
+        send(SCATTER, sum_rep, grad_dev, off)
+    receive(SCATTER, sum_rep, grad_dev)
+    grad_dev[me] = sum_rep[me]
+    rows_sum = grad_dev[0]
+    for d in range(1, n):
+        rows_sum = rows_sum + grad_dev[d]
+    sum_dev[...] = rows_sum
+    for off in range(1, n):
+        share(sum_dev, grad_rows, peer(off), me).start()
+    grad_rows[me] = rows_sum
+    for off in range(1, n):
+        share(sum_dev, grad_rows, peer(off), peer(off)).wait_recv()
+    for off in range(1, reps):
+        across(1, grad_rows, grad_all, rep_peer(off), my_rep).start()
+    grad_all[my_rep] = grad_rows[...]
+    for off in range(1, reps):
+        across(1, grad_rows, grad_all, rep_peer(off), rep_peer(off)).wait_recv()
+    grad_out[...] = grad_all[...]
+
+    finish(ASK, pulls, asked)
+    finish(MOVE_X, send_x, own_x)
+    finish(MOVE_H, send_h, own_h)
+    finish(FAR_X, send_far_x, far_x)
+    finish(FAR_H, send_far_h, far_h)
+    finish(PUSH_ONE, send_one, push_one)
+    finish(PUSH_TWO, send_two, push_two)
+    finish(SCATTER, sum_rep, grad_dev)
+    for off in range(1, n):
+        share(sum_dev, grad_rows, peer(off), me).wait_send()
+    for off in range(1, reps):
+        to = rep_peer(off)
+        across(0, grad_mine.at[to], grad_rep, to, my_rep).wait_send()
+        across(1, grad_rows, grad_all, to, my_rep).wait_send()
+
+
+def fused(
+    features,
+    history,
+    new_owner,
+    pull_rows,
+    occupancy,
+    adj_local,
+    adj_boundary,
+    w_first,
+    bias_first,
+    w_second,
+    cotangent,
+):
+    n, reps = lax.axis_size("dev"), lax.axis_size("rep")
+    height, breadth = features.shape
+    cluster = height // n
+    pulled = pull_rows.shape[0]
+    per_peer = pulled // n
+    part = breadth // (n * reps)
+    vmem = pl.BlockSpec(memory_space=pltpu.VMEM)
+    smem = pl.BlockSpec(memory_space=pltpu.SMEM)
+    anywhere = pl.BlockSpec(memory_space=pl.ANY)
+    moved = pltpu.VMEM((n, cluster, breadth), BF16)
+    listed = pltpu.VMEM((n, per_peer, breadth), BF16)
+    strip = pltpu.VMEM((n, part, breadth), F32)
+    square = pltpu.VMEM((reps, n, part, breadth), F32)
+    hidden, output, gradient = pl.pallas_call(
+        functools.partial(step_kernel, n, reps),
+        out_shape=(
+            jax.ShapeDtypeStruct((height, breadth), BF16),
+            jax.ShapeDtypeStruct((height, breadth), BF16),
+            jax.ShapeDtypeStruct((reps, n, part, breadth), F32),
+        ),
+        in_specs=[
+            vmem,
+            vmem,
+            smem,
+            vmem,
+            smem,
+            anywhere,
+            anywhere,
+            vmem,
+            vmem,
+            vmem,
+            anywhere,
+        ],
+        out_specs=(vmem, vmem, vmem),
+        scratch_shapes=[
+            pltpu.VMEM((height, height), BF16),
+            pltpu.VMEM((height, pulled), BF16),
+            pltpu.VMEM((pulled, height), BF16),
+            pltpu.VMEM((height, breadth), BF16),
+            pltpu.VMEM((n, 1, per_peer), jnp.int32),
+            pltpu.VMEM((height, pulled), BF16),
+            pltpu.VMEM((pulled, height), BF16),
+            moved,
+            moved,
+            moved,
+            moved,
+            listed,
+            listed,
+            listed,
+            listed,
+            listed,
+            listed,
+            listed,
+            listed,
+            pltpu.VMEM((height, breadth), F32),
+            pltpu.VMEM((height, breadth), BF16),
+            pltpu.VMEM((height, breadth), BF16),
+            square,
+            square,
+            strip,
+            strip,
+            pltpu.VMEM((part, breadth), F32),
+            strip,
+            square,
+            pltpu.SemaphoreType.DMA((3,)),
+            pltpu.SemaphoreType.DMA((9, n)),
+            pltpu.SemaphoreType.DMA((9, n)),
+            pltpu.SemaphoreType.DMA((2, reps)),
+            pltpu.SemaphoreType.DMA((2, reps)),
+        ],
+        compiler_params=pltpu.CompilerParams(
+            collective_id=0, has_side_effects=True, vmem_limit_bytes=56 * 1024 * 1024
+        ),
+    )(
+        features,
+        history,
+        new_owner,
+        pull_rows.reshape(n, 1, per_peer),
+        occupancy,
+        adj_local,
+        adj_boundary,
+        w_first,
+        bias_first.reshape(1, breadth),
+        w_second,
+        cotangent,
+    )
+    return hidden, output, gradient.reshape(breadth, breadth)
+
+
+def fits(peers, height, pulled, breadth, everyone):
+    return (
+        height % (128 * peers) == 0 and pulled == 128 * peers and breadth % (8 * everyone) == 0
+    )
 
 
 def expand(occupied):
@@ -39,6 +458,21 @@
     cluster = height // peer_count
     pulled = pull_rows.shape[0]
     per_peer = pulled // peer_count
+    everyone = peer_count * lax.axis_size("rep")
+    if fits(peer_count, height, pulled, breadth, everyone):
+        return fused(
+            features,
+            history,
+            new_owner,
+            pull_rows,
+            occupancy,
+            adj_local,
+            adj_boundary,
+            w_first,
+            bias_first,
+            w_second,
+            cotangent,
+        )
     indices = jnp.arange(peer_count, dtype=jnp.int32)
     matches = (new_owner[0][:, None] == indices[None, :]).astype(jnp.int32)
     inverse = jnp.sum(matches * indices[:, None], axis=0)
@@ -103,7 +537,14 @@
     local_grad = lax.dot_general(
         aggregate_two, cotangent, (((0,), (0,)), ((), ())), preferred_element_type=jnp.float32
     )
-    gradient = lax.psum(local_grad, ("dev", "rep"))
+    slices = lax.all_to_all(
+        local_grad.reshape(everyone, breadth // everyone, breadth),
+        ("dev", "rep"),
+        split_axis=0,
+        concat_axis=0,
+        tiled=True,
+    )
+    gradient = lax.all_gather(jnp.sum(slices, axis=0), ("dev", "rep"), axis=0, tiled=True)
     return (hidden, output, gradient)
 
 

time: 264 us -> 100 us (0.38)
  waiting for transfers between devices: 170 us -> 0 us
  Pallas kernels: 0 us -> 94.8 us
  starting transfers between devices: 31 us -> 0 us
  matrix products: 23.5 us -> 0 us
  local copies, waits for them, and re-layouts: 23.5 us -> 4.48 us
  between operations: 14.2 us -> 0.65 us
    psum x1 -> x0, waiting for transfers between devices: 125 us -> none  [body(): gradient = lax.psum(local_grad, ('dev', 'rep'))]
    pallas_call x0 -> x1, Pallas kernels: none -> 94.8 us  [fused(): pl.pallas_call(functools.partial(step_kernel, n, reps), out_shape=(jax.Sh...]
    all_to_all x7 -> x0, waiting for transfers between devices: 45.4 us -> none  [the longest x1 11.9 us: body(): lax.all_to_all(arrange(features), 'dev', split_axis=0, concat_axis=0, til...]
    all_to_all x7 -> x0, starting transfers between devices: 30.7 us -> none  [the longest x1 7.45 us: body(): lax.all_to_all(pull_rows.reshape(peer_count, per_peer), 'dev', split_axis...]
    dot_general x10 -> x0, matrix products: 23.5 us -> none  [the longest x2 6.92 us: dense_terms(): summed = jnp.dot(local_tile, owned, preferred_element_type=jnp.float32)]
    gather x4 -> x0, local copies, waits for them, and re-layouts: 13.5 us -> none  [the longest x2 10.7 us: fetch_rows(): return values[requests].reshape(peer_count, per_peer, breadth)]
    broadcast_in_dim x2 -> x0, local copies, waits for them, and re-layouts: 4.5 us -> none  [the longest x1 4.46 us: expand(): jnp.repeat(jnp.repeat(occupied, 128, axis=0), 128, axis=1)]
    unnamed x22 -> x5, local copies, waits for them, and re-layouts: 5.58 us -> 4.48 us
  transfers between devices with their start and end apart: 8 -> 0, of which waited for: 8 -> 0; matrix products, arithmetic and copies ran while one was open for 16% -> 0% of each run, Pallas kernels for 0% -> 0%
where the time goes in v1:
time: 100 us; the launch traced here: 99.9 us
  Pallas kernels  94.8 us (95%)
  local copies, waits for them, and re-layouts  4.48 us (4%)
    pallas_call x1, Pallas kernels, fused(): pl.pallas_call(functools.partial(step_kernel, n, reps), out_shape=(jax.Sh...  94.8 us
    unnamed x5, local copies, waits for them, and re-layouts  4.48 us

profile of v1, /device:TPU:0, one launch (start us, length us, event | category | flops | bytes accessed | tf_op | source)
XLA Modules:
  0.0 99.9 jit_solution(6996259685583810523)
XLA Ops:
  0.6 94.8 %shard_map.130 = (bf16[1024,256]{1,0:T(8,128)(2,1)}, bf16[1024,256]{1,0:T(8,128)(2,1)}, f32[4,8,8,256]{3,2,1,0:T(8,128)}) custom-call(bf16[1024,256]{1,0:T(8,128)(2,1)} %features.1, bf16[1024,256]{1,0:T(8,128)(2,1)} %history.1, s32[1,8]{1,0:T(1,128)} %new_owner.1, s32[8,1,128]{2,1,0:T(1,128)} %bitcast.4, s32[8,16]{1,0:T(8,128)} %occupancy.1, ...), custom_call_target="tpu_custom_call" | custom-call | tf_op jit(solution)/shard_map/pallas_call | solution.py:344
  95.4 0.0 copy-start
  95.4 1.9 %copy.17 = bf16[1024,256]{1,0:T(8,128)(2,1)} copy(bf16[1024,256]{1,0:T(8,128)(2,1)} %get-tuple-element.12) | data formatting | bytes 1048576
  97.3 1.9 %copy.18 = bf16[1024,256]{1,0:T(8,128)(2,1)} copy(bf16[1024,256]{1,0:T(8,128)(2,1)} %get-tuple-element.13) | data formatting | bytes 1048576
  99.2 0.0 copy-done
  99.2 0.7 copy.19
Async XLA Ops:
  95.4 3.8 %copy-start = (f32[4,8,8,256]{3,2,1,0:T(8,128)S(1)}, f32[4,8,8,256]{3,2,1,0:T(8,128)}, u32[]{:S(2)}) copy-start(f32[4,8,8,256]{3,2,1,0:T(8,128)} %get-tuple-element.8) | copy-start | bytes 786436

commit v2 on v1

--- a/solution.py
+++ b/solution.py
@@ -17,7 +17,7 @@
     n,
     reps,
     features,
-    history,
+    history_hbm,
     new_owner,
     pulls,
     occupancy,
@@ -25,11 +25,11 @@
     adj_edge_hbm,
     w_first,
     bias_first,
-    w_second,
     cotangent_hbm,
-    hidden_out,
-    output_out,
+    pre_out,
+    agg_out,
     grad_out,
+    history,
     local,
     edge,
     edge_t,
@@ -50,6 +50,7 @@
     push_one,
     push_two,
     acc,
+    pre,
     hidden,
     agg,
     grad_mine,
@@ -74,8 +75,10 @@
     tile = height // occupancy.shape[0]
     band = min(256, height)
 
+    side = 1 - 2 * (me // (n // 2))
+
     def peer(off):
-        return lax.rem(me + off, n)
+        return lax.rem(me + side * off + n, n)
 
     def rep_peer(off):
         return lax.rem(my_rep + off, reps)
@@ -84,9 +87,10 @@
         pltpu.make_async_copy(adj_edge_hbm, edge, load_sem.at[0]),
         pltpu.make_async_copy(adj_local_hbm, local, load_sem.at[1]),
         pltpu.make_async_copy(cotangent_hbm, cotangent, load_sem.at[2]),
+        pltpu.make_async_copy(history_hbm, history, load_sem.at[3]),
     ]
-    for load in loads:
-        load.start()
+    for k in (3, 0, 1, 2):
+        loads[k].start()
 
     barrier = pltpu.get_barrier_semaphore()
     for off in range(1, n):
@@ -132,6 +136,7 @@
         send(ASK, pulls, asked, off)
     for off in range(1, n):
         send(MOVE_X, send_x, own_x, off)
+    loads[3].wait()
     for off in range(1, n):
         send_h[peer(off)] = cluster_for(history, peer(off))
         send(MOVE_H, send_h, own_h, off)
@@ -214,12 +219,13 @@
     def first(rows):
         total = (acc[rows, :] + times(pick, rows, push_one)).astype(BF16)
         value = jnp.dot(total, w_first[...], preferred_element_type=F32) + bias_first[...]
-        value = jnp.maximum(value, 0.0).astype(BF16)
-        hidden[rows, :] = value
-        hidden_out[rows, :] = value
+        pre[rows, :] = value.astype(BF16)
+        hidden[rows, :] = jnp.maximum(value, 0.0).astype(BF16)
 
     bands(first)
     blocks_out(PUSH_TWO, edge_t, hidden, send_two, push_two)
+    store_pre = pltpu.make_async_copy(pre, pre_out, load_sem.at[0])
+    store_pre.start()
 
     def local_two(rows):
         acc[rows, :] = times(local, rows, hidden)
@@ -238,17 +244,18 @@
         agg[rows, :] = (acc[rows, :] + times(pick, rows, push_two)).astype(BF16)
 
     bands(second)
+    store_agg = pltpu.make_async_copy(agg, agg_out, load_sem.at[1])
     grad = lax.dot_general(
         agg[...], cotangent[...], (((0,), (0,)), ((), ())), preferred_element_type=F32
     )
     grad_mine[...] = grad.reshape(grad_mine.shape)
 
-    def across(phase, src, dst, to, slot):
+    def across(phase, src, dst, to, slot, piece):
         return pltpu.make_async_remote_copy(
             src_ref=src,
-            dst_ref=dst.at[slot],
-            send_sem=rep_send.at[phase, to],
-            recv_sem=rep_recv.at[phase, slot],
+            dst_ref=dst.at[slot, piece],
+            send_sem=rep_send.at[phase, to, piece],
+            recv_sem=rep_recv.at[phase, slot, piece],
             device_id={"rep": to},
             device_id_type=MESH,
         )
@@ -263,42 +270,49 @@
             device_id_type=MESH,
         )
 
-    for off in range(1, reps):
-        to = rep_peer(off)
-        across(0, grad_mine.at[to], grad_rep, to, my_rep).start()
-
-    def last(rows):
-        output_out[rows, :] = jnp.dot(
-            agg[rows, :], w_second[...], preferred_element_type=F32
-        ).astype(BF16)
-
-    bands(last)
-    total = grad_mine[my_rep]
-    for off in range(1, reps):
-        to = rep_peer(off)
-        across(0, grad_mine.at[to], grad_rep, to, to).wait_recv()
-        total = total + grad_rep[to]
-    sum_rep[...] = total
-    for off in range(1, n):
-        send(SCATTER, sum_rep, grad_dev, off)
+    order = list(range(n - 1, -1, -1))
+    for off in order:
+        piece = peer(off)
+        for step in range(1, reps):
+            to = rep_peer(step)
+            across(0, grad_mine.at[to, piece], grad_rep, to, my_rep, piece).start()
+    store_agg.start()
+    for off in order:
+        piece = peer(off)
+        total = grad_mine[my_rep, piece]
+        for step in range(1, reps):
+            to = rep_peer(step)
+            across(0, grad_mine.at[to, piece], grad_rep, to, to, piece).wait_recv()
+            total = total + grad_rep[to, piece]
+        sum_rep[piece] = total
+        if off > 0:
+            send(SCATTER, sum_rep, grad_dev, off)
     receive(SCATTER, sum_rep, grad_dev)
     grad_dev[me] = sum_rep[me]
     rows_sum = grad_dev[0]
     for d in range(1, n):
         rows_sum = rows_sum + grad_dev[d]
     sum_dev[...] = rows_sum
-    for off in range(1, n):
+    for off in order[:-1]:
         share(sum_dev, grad_rows, peer(off), me).start()
-    grad_rows[me] = rows_sum
-    for off in range(1, n):
-        share(sum_dev, grad_rows, peer(off), peer(off)).wait_recv()
-    for off in range(1, reps):
-        across(1, grad_rows, grad_all, rep_peer(off), my_rep).start()
-    grad_all[my_rep] = grad_rows[...]
-    for off in range(1, reps):
-        across(1, grad_rows, grad_all, rep_peer(off), rep_peer(off)).wait_recv()
+    for step in range(1, reps):
+        across(1, sum_dev, grad_all, rep_peer(step), my_rep, me).start()
+    grad_all[my_rep, me] = rows_sum
+    for off in range(1, n):
+        piece = peer(off)
+        share(sum_dev, grad_rows, piece, piece).wait_recv()
+        for step in range(1, reps):
+            across(1, grad_rows.at[piece], grad_all, rep_peer(step), my_rep, piece).start()
+        grad_all[my_rep, piece] = grad_rows[piece]
+    for off in range(n):
+        piece = peer(off)
+        for step in range(1, reps):
+            to = rep_peer(step)
+            across(1, grad_rows.at[piece], grad_all, to, to, piece).wait_recv()
     grad_out[...] = grad_all[...]
 
+    store_pre.wait()
+    store_agg.wait()
     finish(ASK, pulls, asked)
     finish(MOVE_X, send_x, own_x)
     finish(MOVE_H, send_h, own_h)
@@ -309,10 +323,12 @@
     finish(SCATTER, sum_rep, grad_dev)
     for off in range(1, n):
         share(sum_dev, grad_rows, peer(off), me).wait_send()
-    for off in range(1, reps):
-        to = rep_peer(off)
-        across(0, grad_mine.at[to], grad_rep, to, my_rep).wait_send()
-        across(1, grad_rows, grad_all, to, my_rep).wait_send()
+    for off in range(n):
+        piece = peer(off)
+        for step in range(1, reps):
+            to = rep_peer(step)
+            across(0, grad_mine.at[to, piece], grad_rep, to, my_rep, piece).wait_send()
+            across(1, grad_rows.at[piece], grad_all, to, my_rep, piece).wait_send()
 
 
 def fused(
@@ -341,7 +357,7 @@
     listed = pltpu.VMEM((n, per_peer, breadth), BF16)
     strip = pltpu.VMEM((n, part, breadth), F32)
     square = pltpu.VMEM((reps, n, part, breadth), F32)
-    hidden, output, gradient = pl.pallas_call(
+    pre, agg, gradient = pl.pallas_call(
         functools.partial(step_kernel, n, reps),
         out_shape=(
             jax.ShapeDtypeStruct((height, breadth), BF16),
@@ -350,7 +366,7 @@
         ),
         in_specs=[
             vmem,
-            vmem,
+            anywhere,
             smem,
             vmem,
             smem,
@@ -358,11 +374,11 @@
             anywhere,
             vmem,
             vmem,
-            vmem,
             anywhere,
         ],
-        out_specs=(vmem, vmem, vmem),
+        out_specs=(anywhere, anywhere, vmem),
         scratch_shapes=[
+            pltpu.VMEM((height, breadth), BF16),
             pltpu.VMEM((height, height), BF16),
             pltpu.VMEM((height, pulled), BF16),
             pltpu.VMEM((pulled, height), BF16),
@@ -385,6 +401,7 @@
             pltpu.VMEM((height, breadth), F32),
             pltpu.VMEM((height, breadth), BF16),
             pltpu.VMEM((height, breadth), BF16),
+            pltpu.VMEM((height, breadth), BF16),
             square,
             square,
             strip,
@@ -392,11 +409,11 @@
             pltpu.VMEM((part, breadth), F32),
             strip,
             square,
-            pltpu.SemaphoreType.DMA((3,)),
+            pltpu.SemaphoreType.DMA((4,)),
             pltpu.SemaphoreType.DMA((9, n)),
             pltpu.SemaphoreType.DMA((9, n)),
-            pltpu.SemaphoreType.DMA((2, reps)),
-            pltpu.SemaphoreType.DMA((2, reps)),
+            pltpu.SemaphoreType.DMA((2, reps, n)),
+            pltpu.SemaphoreType.DMA((2, reps, n)),
         ],
         compiler_params=pltpu.CompilerParams(
             collective_id=0, has_side_effects=True, vmem_limit_bytes=56 * 1024 * 1024
@@ -411,9 +428,10 @@
         adj_boundary,
         w_first,
         bias_first.reshape(1, breadth),
-        w_second,
         cotangent,
     )
+    hidden = jnp.maximum(pre, jnp.zeros((), BF16))
+    output = jnp.dot(agg, w_second, preferred_element_type=F32).astype(BF16)
     return hidden, output, gradient.reshape(breadth, breadth)
 
 

time: 100 us -> 100 us (level)
  local copies, waits for them, and re-layouts: 4.48 us -> 0.72 us
  matrix products: 0 us -> 2.14 us
  other arithmetic: 0 us -> 1.91 us
    unnamed x5, local copies, waits for them, and re-layouts: 4.48 us -> 0.72 us
    dot_general x0 -> x1, matrix products: none -> 2.14 us  [fused(): output = jnp.dot(agg, w_second, preferred_element_type=F32).astype(BF16)]
    max x0 -> x1, other arithmetic: none -> 1.91 us  [fused(): hidden = jnp.maximum(pre, jnp.zeros((), BF16))]
where the time goes in v2:
time: 100 us
  Pallas kernels  94.7 us (95%)
  matrix products  2.14 us (2%)
  other arithmetic  1.91 us (2%)
    pallas_call x1, Pallas kernels, fused(): pl.pallas_call(functools.partial(step_kernel, n, reps), out_shape=(jax.Sh...  94.7 us
    dot_general x1, matrix products, fused(): output = jnp.dot(agg, w_second, preferred_element_type=F32).astype(BF16)  2.14 us

profile of v2, /device:TPU:0, one launch (start us, length us, event | category | flops | bytes accessed | tf_op | source)
XLA Modules:
  0.0 100.1 jit_solution(943504181679205094)
XLA Ops:
  0.6 0.0 copy-start
  0.6 94.7 %shard_map.130 = (bf16[1024,256]{1,0:T(8,128)(2,1)}, bf16[1024,256]{1,0:T(8,128)(2,1)}, f32[4,8,8,256]{3,2,1,0:T(8,128)}) custom-call(bf16[1024,256]{1,0:T(8,128)(2,1)} %features.1, bf16[1024,256]{1,0:T(8,128)(2,1)} %history_hbm.1, s32[1,8]{1,0:T(1,128)} %new_owner.1, s32[8,1,128]{2,1,0:T(1,128)} %bitcast.6, s32[8,16]{1,0:T(8,128)} %occupancy.1, ...), custom_call_target="tpu_custom_call" | custom-call | tf_op jit(solution)/shard_map/pallas_call | solution.py:360
  95.3 0.0 copy-start.1
  95.3 1.9 %broadcast_maximum_fusion = bf16[1024,256]{1,0:T(8,128)(2,1)} fusion(bf16[1024,256]{1,0:T(8,128)(2,1)} %get-tuple-element.6), kind=kLoop, calls=%fused_computation.1 | loop fusion | flops 262144 | bytes 1048576 | tf_op jit(solution)/shard_map/max | solution.py:433
  97.2 0.0 copy-done
  97.2 2.1 %convolution_convert_fusion = bf16[1024,256]{1,0:T(8,128)(2,1)} fusion(bf16[1024,256]{1,0:T(8,128)(2,1)} %get-tuple-element.7, bf16[256,256]{1,0:T(8,128)(2,1)S(1)} %copy-done), kind=kOutput, calls=%fused_computation | convolution fusion | flops 134479872 | bytes 1179648 | tf_op jit(solution)/shard_map/dot_general | solution.py:434
  99.4 0.0 copy-done.1
  99.4 0.7 copy.15
Async XLA Ops:
  0.6 96.6 %copy-start = (bf16[256,256]{1,0:T(8,128)(2,1)S(1)}, bf16[256,256]{1,0:T(8,128)(2,1)}, u32[]{:S(2)}) copy-start(bf16[256,256]{1,0:T(8,128)(2,1)} %param.20) | copy-start | bytes 393220
  95.3 4.1 %copy-start.1 = (f32[4,8,8,256]{3,2,1,0:T(8,128)S(1)}, f32[4,8,8,256]{3,2,1,0:T(8,128)}, u32[]{:S(2)}) copy-start(f32[4,8,8,256]{3,2,1,0:T(8,128)} %get-tuple-element.8) | copy-start | bytes 786436
